TPU v7x, 32 devices: a whole 2x2x4 slice. The times are simulated.
32 devices in a mesh: ens: 4 (over x, core), dp: 8 (over z, y).
Axes of the slice: x: 2, y: 2, z: 4, core: 2. Of those that a mesh axis runs over, the one named last changes fastest.
Arguments:
- features: bfloat16 [3072, 256], P('dp'), may hold values from -4 to 4
- reward: float32 [3072], P('dp'), may hold values from -16 to 16
- done: int32 [3072], P('dp'), may hold values 0 or 1
- value_next: float32 [3072], P('dp'), may hold values from -16 to 16
- value_now: float32 [3072], P('dp'), may hold values from -4 to 4
- w_in: bfloat16 [8, 256, 2048], P('ens'), may hold values from -0.375 to 0.375
- w_mid: bfloat16 [8, 2048, 2048], P('ens'), may hold values from -0.099121094 to 0.099121094
- biases: float32 [2, 8, 2048], P(None, 'ens'), may hold values from -3 to 3
- w_out: bfloat16 [8, 2048], P('ens'), may hold values from -0.011048543 to 0.011048543
Outputs:
- value_grad: float32 [3072], P('dp')
- d_in: float32 [256, 8, 2048], P('dp', 'ens')
- d_mid: float32 [2048, 8, 2048], P('dp', 'ens')
- d_bias: float32 [2, 8, 2048], P(None, 'ens', 'dp')
- d_out: float32 [8, 2048], P('ens', 'dp')
All inputs are finite; a program needn't handle non-finite values. No bound on the sum of `done` on one device may be relied on, other than what follows from the above.
Results may differ from a plain program's by a relative error of at most 0.013.
Values may be sent and summed in bfloat16 or wider, within the bound.
A program may use at most 128 MiB of HBM per device.

v0:
```python
import jax
import jax.numpy as jnp
from jax import lax
from jax.sharding import PartitionSpec as P


def silu_slope(value):
    sig = jax.nn.sigmoid(value)
    return sig * (1.0 + value * (1.0 - sig))


def per_device(features, reward, done, value_next, value_now, w_in, w_mid, biases, w_out):
    high = lax.Precision.HIGHEST
    pre_one = (
        jnp.einsum("ra,hak->hrk", features, w_in, preferred_element_type=jnp.float32)
        + biases[0][:, None, :]
    )
    act_one = jax.nn.silu(pre_one).astype(jnp.bfloat16)
    pre_two = (
        jnp.einsum("hrk,hkj->hrj", act_one, w_mid, preferred_element_type=jnp.float32)
        + biases[1][:, None, :]
    )
    act_two = jax.nn.silu(pre_two).astype(jnp.bfloat16)
    q_values = jnp.einsum("hrj,hj->hr", act_two, w_out, preferred_element_type=jnp.float32)
    q_min = lax.pmin(jnp.min(q_values, axis=0), "ens")
    gap = q_min - value_now
    weight = jnp.where(gap < 0.0, 0.3, 0.7)
    value_grad = -2.0 * weight * gap
    target = reward + 0.99 * (1.0 - done.astype(jnp.float32)) * value_next
    error = q_values - target[None, :]
    delta_two = (
        error[:, :, None] * w_out.astype(jnp.float32)[:, None, :] * silu_slope(pre_two)
    ).astype(jnp.bfloat16)
    grad_out = jnp.einsum(
        "hr,hrj->hj", error, act_two, preferred_element_type=jnp.float32, precision=high
    )
    grad_two = jnp.sum(delta_two.astype(jnp.float32), axis=1)
    back = jnp.einsum("hrj,hkj->hrk", delta_two, w_mid, preferred_element_type=jnp.float32)
    delta_one = (back * silu_slope(pre_one)).astype(jnp.bfloat16)
    grad_in = jnp.einsum("ra,hrk->ahk", features, delta_one, preferred_element_type=jnp.float32)
    grad_one = jnp.sum(delta_one.astype(jnp.float32), axis=1)
    grad_in, grad_bias = (grad_in, jnp.stack([grad_one, grad_two]))
    grad_mid = jnp.einsum("hrk,hrj->khj", act_one, delta_two, preferred_element_type=jnp.float32)
    d_in, d_mid, d_bias, d_out = (
        lax.psum_scatter(
            grad_in.astype(jnp.bfloat16), "dp", scatter_dimension=0, tiled=True
        ).astype(jnp.float32),
        lax.psum_scatter(
            grad_mid.astype(jnp.bfloat16), "dp", scatter_dimension=0, tiled=True
        ).astype(jnp.float32),
        lax.psum_scatter(
            grad_bias.astype(jnp.bfloat16), "dp", scatter_dimension=2, tiled=True
        ).astype(jnp.float32),
        lax.psum_scatter(
            grad_out.astype(jnp.bfloat16), "dp", scatter_dimension=1, tiled=True
        ).astype(jnp.float32),
    )
    return (value_grad, d_in, d_mid, d_bias, d_out)


def solution(mesh):
    in_specs = (
        P("dp", None),
        P("dp"),
        P("dp"),
        P("dp"),
        P("dp"),
        P("ens", None, None),
        P("ens", None, None),
        P(None, "ens", None),
        P("ens", None),
    )
    out_specs = (
        P("dp"),
        P("dp", "ens", None),
        P("dp", "ens", None),
        P(None, "ens", "dp"),
        P("ens", "dp"),
    )
    return jax.shard_map(
        per_device, mesh=mesh, in_specs=in_specs, out_specs=out_specs, check_vma=False
    )
```

profile of v0, /device:TPU:0, one launch (start us, length us, event | category | flops | bytes accessed | tf_op | source)
XLA Modules:
  0.0 561.3 jit_solution(7664245751138094531)
XLA Ops:
  7.2 0.9 slice_bitcast_fusion
  8.1 0.7 copy-done
  8.8 1.9 fusion.10
  10.8 14.9 %multiply_convert_fusion.1 = (bf16[2,384,2048]{2,1,0:T(8,128)(2,1)S(1)}, f32[2,384,2048]{2,1,0:T(8,128)}) fusion(f32[2,2048]{1,0:T(2,128)S(1)} %get-tuple-element.17, bf16[2,2048,2048]{2,1,0:T(8,128)(2,1)} %param.15, f32[2,2048,384]{1,2,0:T(8,128)S(1)} %fusion.10, f32[2,2048]{1,0:T(2,128)S(1)} %get-tuple-element.18), kind=kOutput, calls=%fused_computation.13 | convolution fusion | flops 6461325312 | bytes 32538624 | tf_op jit(solution)/shard_map/hrk,hkj->hrj/dot_general | solution.py:20
  25.7 0.9 fusion.12
  26.7 1.3 fusion.14
  28.0 1.1 copy.30
  29.1 0.0 reduce-scatter.10.cloned.1.call-start
  29.2 5.7 %fusion.19 = (bf16[2,2048]{1,0:T(2,128)(2,1)S(1)}, bf16[2,384,2048]{2,1,0:T(8,128)(2,1)}) fusion(f32[2,384,2048]{2,1,0:T(8,128)} %get-tuple-element.22, f32[2,2048]{1,0:T(2,128)S(1)} %get-tuple-element.17, f32[2,2048]{1,0:T(2,128)S(1)} %convert_element_type.55, f32[2,384]{1,0:T(2,128)S(1)} %get-tuple-element.19), kind=kLoop, calls=%fused_computation.34 | loop fusion | flops 18870272 | bytes 9481216 | tf_op jit(solution)/shard_map/reduce_sum | solution.py:37
  34.9 14.7 %fusion.20 = (bf16[2,2048]{1,0:T(2,128)(2,1)S(1)}, bf16[2,384,2048]{2,1,0:T(8,128)(2,1)}) fusion(f32[2,2048,384]{1,2,0:T(8,128)} %copy-done.2, f32[2,2048]{1,0:T(2,128)S(1)} %get-tuple-element.18, bf16[2,384,2048]{2,1,0:T(8,128)(2,1)} %get-tuple-element.16, bf16[2,2048,2048]{2,1,0:T(8,128)(2,1)} %param.15), kind=kOutput, calls=%fused_computation.35 | convolution fusion | flops 6459748352 | bytes 29384704 | tf_op jit(solution)/shard_map/hrj,hkj->hrk/dot_general | solution.py:38
  49.6 0.9 copy.28
  50.5 1.3 reshape.20
  51.9 0.2 all-reduce.3.cloned.1.call-start
  52.1 3.2 fusion.8
  55.3 4.1 copy.19
  59.4 0.0 reduce-scatter.8.cloned.1.call-start
  59.5 15.8 %convert_bitcast_fusion = bf16[2048,2,2048]{0,2,1:T(8,128)(2,1)} fusion(bf16[2,384,2048]{2,1,0:T(8,128)(2,1)} %get-tuple-element.16, f32[2,2048,384]{1,2,0:T(8,128)} %copy-done.2, f32[2,2048]{1,0:T(2,128)S(1)} %get-tuple-element.18), kind=kOutput, calls=%fused_computation | convolution fusion | flops 6460276736 | bytes 26230784 | tf_op jit(solution)/shard_map/hrk,hrj->khj/dot_general | solution.py:43
  75.3 0.6 copy-done.9
  76.0 0.6 dynamic-slice
  77.2 8.3 %pmin.7 = f32[384]{0:T(512)S(1)} all-reduce(f32[384]{0:T(512)S(1)} %get-tuple-element.20), channel_id=1, replica_groups=mesh['ens'=4,'dp'=8] {'ens'}, use_global_device_ids=true, to_apply=%region_1.2 | all-reduce | flops 384 | bytes 3072 | tf_op jit(solution)/shard_map/pmin | solution.py:25
  85.5 0.6 multiply_multiply_fusion
  86.1 8.5 %reduce-scatter.12.cloned.1.call-done = bf16[256,2]{1,0:T(8,128)(2,1)} async-done(((bf16[2048,2]{1,0:T(8,128)(2,1)}), bf16[256,2]{1,0:T(8,128)(2,1)}) %reduce-scatter.12.cloned.1.call-update) | async-done | bytes 1040
  94.6 0.9 copy.31
  95.5 0.6 convert_element_type.68
  96.2 64.1 %reduce-scatter.10.cloned.1.call-done = bf16[256,4]{1,0:T(8,128)(2,1)} async-done(((bf16[2048,4]{1,0:T(8,128)(2,1)}), bf16[256,4]{1,0:T(8,128)(2,1)}) %reduce-scatter.10.cloned.1.call-update) | async-done | bytes 2064
  160.3 0.9 reshape.21
  161.2 0.1 copy.29
  161.3 0.6 convert_element_type.66
  161.9 103.3 %all-reduce.3.cloned.1.call-done = bf16[256,2,2048]{2,1,0:T(2,128)(2,1)} async-done(((bf16[256,2,2048]{2,1,0:T(2,128)(2,1)}), bf16[256,2,2048]{2,1,0:T(2,128)(2,1)}) %all-reduce.3.cloned.1.call-update) | async-done | bytes 2097168
  265.2 2.0 dynamic-slice_convert_fusion
  267.2 281.2 %reduce-scatter.8.cloned.1.call-done = bf16[256,2,2048]{0,2,1:T(8,128)(2,1)} async-done(((bf16[2048,2,2048]{0,2,1:T(8,128)(2,1)}), bf16[256,2,2048]{0,2,1:T(8,128)(2,1)}) %reduce-scatter.8.cloned.1.call-update) | async-done | bytes 2097168 | tf_op jit(solution)/shard_map/reduce_scatter | solution.py:48
  548.4 6.4 %copy.21 = f32[256,2,2048]{2,1,0:T(2,128)} copy(bf16[256,2,2048]{0,2,1:T(8,128)(2,1)} %reduce-scatter.8.cloned.1.call-done) | data formatting | bytes 6291456
  (28 shorter events, 0.2 us)
Async XLA Ops:
  7.2 1.6 copy-start
  7.2 87.5 %reduce-scatter.12.cloned.1.call-start = ((), (), s32[]{:S(2)}) async-start(), calls=%async_computation.5 | async-start | bytes 589824
  10.7 15.0 %copy-start.2 = (f32[2,2048,384]{1,2,0:T(8,128)}, f32[2,2048,384]{1,2,0:T(8,128)S(1)}, u32[]{:S(2)}) copy-start(f32[2,2048,384]{1,2,0:T(8,128)S(1)} %fusion.10) | copy-start | bytes 18874372
  10.7 15.0 %copy-start.4 = (bf16[2,2048]{1,0:T(2,128)(2,1)S(1)}, bf16[2,2048]{1,0:T(2,128)(2,1)}, u32[]{:S(2)}) copy-start(bf16[2,2048]{1,0:T(2,128)(2,1)} %param.17) | copy-start | bytes 24580
  10.7 15.9 %copy-start.6 = (f32[384]{0:T(512)S(1)}, f32[384]{0:T(512)}, u32[]{:S(2)}) copy-start(f32[384]{0:T(512)} %param.10) | copy-start | bytes 4612
  10.7 15.9 %copy-start.7 = (f32[384]{0:T(512)S(1)}, f32[384]{0:T(512)}, u32[]{:S(2)}) copy-start(f32[384]{0:T(512)} %param.12) | copy-start | bytes 4612
  10.8 15.9 %copy-start.8 = (s32[384]{0:T(512)S(1)}, s32[384]{0:T(512)}, u32[]{:S(2)}) copy-start(s32[384]{0:T(512)} %param.11) | copy-start | bytes 4612
  29.1 131.1 %reduce-scatter.10.cloned.1.call-start = ((), (), s32[]{:S(2)}) async-start(), calls=%async_computation.4 | async-start | bytes 589824
  34.9 17.2 %copy-start.3 = (bf16[384,256]{1,0:T(8,128)(2,1)S(1)}, bf16[384,256]{1,0:T(8,128)(2,1)}, u32[]{:S(2)}) copy-start(bf16[384,256]{1,0:T(8,128)(2,1)} %param.9) | copy-start | bytes 589828
  51.9 213.4 %all-reduce.3.cloned.1.call-start = ((), (), s32[]{:S(2)}) async-start(), calls=%async_computation.6 | async-start | bytes 4194304
  59.4 489.0 %reduce-scatter.8.cloned.1.call-start = ((), (), s32[]{:S(2)}) async-start(), calls=%async_computation.3 | async-start | bytes 18874368 | tf_op jit(solution)/shard_map/reduce_scatter | solution.py:48
  75.3 0.7 copy-start.9
  75.3 10.2 %copy-start.5 = (f32[384]{0:T(512)S(1)}, f32[384]{0:T(512)}, u32[]{:S(2)}) copy-start(f32[384]{0:T(512)} %param.13) | copy-start | bytes 4612
  75.3 479.5 %copy-start.1 = (bf16[2,256,2048]{2,1,0:T(8,128)(2,1)S(1)}, bf16[2,256,2048]{2,1,0:T(8,128)(2,1)}, u32[]{:S(2)}) copy-start(bf16[2,256,2048]{2,1,0:T(8,128)(2,1)} %param.14) | copy-start | bytes 6291460
Sparse Core Ops, SparseCore 0:
  29.2 65.3 reduce-scatter.11
  98.5 61.6 reduce-scatter.9
  163.9 101.2 all-reduce.2
  268.9 279.5 reduce-scatter.7
where the time goes:
time: 562 us; the launch traced here: 561 us
  waiting for transfers between devices  457 us (81%)
  matrix products  52.7 us (9%)
  local copies, waits for them, and re-layouts  18.6 us (3%)
  between operations  14.6 us (3%)
  other arithmetic  9.62 us (2%)
  blocking collectives  8.34 us (1%)
    reduce_scatter x1, waiting for transfers between devices, per_device(): lax.psum_scatter(grad_mid.astype(jnp.bfloat16), 'dp', scatter_dimension=0...  281 us
    unnamed x7, waiting for transfers between devices  176 us
    dot_general x1, matrix products, per_device(): jnp.einsum('hrk,hrj->khj', act_one, delta_two, preferred_element_type=jnp...  15.8 us
    dot_general x1, matrix products, per_device(): jnp.einsum('hrk,hkj->hrj', act_one, w_mid, preferred_element_type=jnp.flo...  14.9 us
    dot_general x1, matrix products, per_device(): jnp.einsum('hrj,hkj->hrk', delta_two, w_mid, preferred_element_type=jnp.f...  14.7 us
    unnamed x28, local copies, waits for them, and re-layouts  13.6 us
  transfers between devices with their start and end apart: 4, of which 4 were waited for; matrix products, arithmetic and copies ran while one was open for 9% of the time, Pallas kernels for 0%

commit v1 on v0

v1 whole, which is shorter than its diff:
```python
import functools

import jax
import jax.numpy as jnp
from jax import lax
from jax.experimental import pallas as pl
from jax.experimental.pallas import tpu as pltpu
from jax.sharding import PartitionSpec as P

MESH = pl.DeviceIdType.MESH


def dot(a, b):
    return jnp.dot(a, b, preferred_element_type=jnp.float32)


def sigmoid(v):
    return 0.5 * jnp.tanh(0.5 * v) + 0.5


def kernel(
    n, e, x_ref, reward_ref, done_ref, vnext_ref, vnow_ref, w_in_ref, w_mid_hbm, bias_ref,
    w_out_ref, vg_ref, din_ref, dmid_ref, dbias_ref, dout_ref,
    w_mid, w_back, x_all, tgt_all, act_s, act2_s, g_s, delta_s, acc_mid, acc_in, stage, ibuf,
    qmin_s, qbuf, w_sem, xs_sem, xr_sem, ts_sem, tr_sem, is_sem, ir_sem, qs_sem, qr_sem,
):
    me = lax.axis_index("dp")
    my_ens = lax.axis_index("ens")
    rows, feats = x_ref.shape
    heads, _, units = w_in_ref.shape
    ks = units // n
    fs = feats // n
    chunk = min(512, units)
    chunks = units // chunk
    mine = pl.ds(pl.multiple_of(me * ks, ks), ks)

    loads = [
        pltpu.make_async_copy(w_mid_hbm.at[h], w_mid.at[h], w_sem.at[h]) for h in range(heads)
    ]
    for load in loads:
        load.start()

    barrier = pltpu.get_barrier_semaphore()
    for d in range(1, n):
        pl.semaphore_signal(
            barrier, inc=1, device_id={"dp": lax.rem(me + d, n)}, device_id_type=MESH
        )
    for d in range(1, e):
        pl.semaphore_signal(
            barrier, inc=1, device_id={"ens": lax.rem(my_ens + d, e)}, device_id_type=MESH
        )
    tgt_all[0] = reward_ref[...] + 0.99 * (1.0 - done_ref[...].astype(jnp.float32)) * vnext_ref[...]
    x_all[0] = x_ref[...]
    acc_mid[...] = jnp.zeros_like(acc_mid)
    acc_in[...] = jnp.zeros_like(acc_in)
    dbias_ref[...] = jnp.zeros_like(dbias_ref)
    dout_ref[...] = jnp.zeros_like(dout_ref)
    pl.semaphore_wait(barrier, n + e - 2)

    def send_x(d):
        return pltpu.make_async_remote_copy(
            src_ref=x_ref, dst_ref=x_all.at[d], send_sem=xs_sem.at[d], recv_sem=xr_sem.at[d],
            device_id={"dp": lax.rem(me + d, n)}, device_id_type=MESH,
        )

    def send_t(d):
        return pltpu.make_async_remote_copy(
            src_ref=tgt_all.at[0], dst_ref=tgt_all.at[d], send_sem=ts_sem.at[d],
            recv_sem=tr_sem.at[d], device_id={"dp": lax.rem(me + d, n)}, device_id_type=MESH,
        )

    def send_q(d):
        return pltpu.make_async_remote_copy(
            src_ref=qmin_s, dst_ref=qbuf.at[d], send_sem=qs_sem.at[d], recv_sem=qr_sem.at[d],
            device_id={"ens": lax.rem(my_ens + d, e)}, device_id_type=MESH,
        )

    def send_in(d):
        peer = lax.rem(me + d, n)
        return pltpu.make_async_remote_copy(
            src_ref=stage.at[:, pl.ds(pl.multiple_of(peer * fs, fs), fs), :],
            dst_ref=ibuf.at[d], send_sem=is_sem.at[d], recv_sem=ir_sem.at[d],
            device_id={"dp": peer}, device_id_type=MESH,
        )

    for d in range(1, n):
        send_x(d).start()
        send_t(d).start()

    diag = lax.broadcasted_iota(jnp.int32, (rows, rows), 0) == lax.broadcasted_iota(
        jnp.int32, (rows, rows), 1
    )

    def step(t, carry):
        @pl.when(t > 0)
        def _():
            send_x(t).wait_recv()
            send_t(t).wait_recv()

        @pl.when(t == 1)
        def _():
            for d in range(1, e):
                send_q(d).start()

        x = x_all[t]
        x_t = x.T
        tgt = jnp.sum(jnp.where(diag, tgt_all[t], 0.0), axis=1, keepdims=True)

        def head(h, carry):
            for c in range(chunks):
                cols = pl.ds(c * chunk, chunk)
                v = dot(x, w_in_ref[h, :, cols]) + bias_ref[0, h, :, cols]
                act_s[:, cols] = (v * sigmoid(v)).astype(jnp.bfloat16)

            @pl.when(t == 0)
            def _():
                pltpu.make_async_copy(w_mid_hbm.at[h], w_mid.at[h], w_sem.at[h]).wait()
                w_back[h] = w_mid[h, mine, :].T

            q = jnp.zeros((rows, 1), jnp.float32)
            for c in range(chunks):
                cols = pl.ds(c * chunk, chunk)
                v = dot(act_s[...], w_mid[h, :, cols]) + bias_ref[1, h, :, cols]
                s = sigmoid(v)
                a = v * s
                rounded = a.astype(jnp.bfloat16)
                act2_s[:, cols] = rounded
                wo = w_out_ref[h, :, cols]
                q += jnp.sum(rounded.astype(jnp.float32) * wo, axis=1, keepdims=True)
                g_s[:, cols] = (s + a * (1.0 - s)) * wo

            @pl.when(t == 0)
            def _():
                q_row = jnp.sum(jnp.where(diag, q, 0.0), axis=0, keepdims=True)
                qmin_s[...] = jnp.where(h == 0, q_row, jnp.minimum(q_row, qmin_s[...]))

            err = q - tgt
            act_t = act_s[:, mine].T
            back = jnp.zeros((rows, ks), jnp.float32)
            for c in range(chunks):
                cols = pl.ds(c * chunk, chunk)
                delta = (err * g_s[:, cols]).astype(jnp.bfloat16)
                delta_s[:, cols] = delta
                back += dot(delta, w_back[h, cols, :])
                acc_mid[h, :, cols] += dot(act_t, delta)
            v = dot(x, w_in_ref[h, :, mine]) + bias_ref[0, h, :, mine]
            s = sigmoid(v)
            delta_one = (back * (s + v * s * (1.0 - s))).astype(jnp.bfloat16)
            acc_in[h] += dot(x_t, delta_one)
            dbias_ref[0, h] += jnp.sum(delta_one.astype(jnp.float32), axis=0, keepdims=True)
            dbias_ref[1, h] += jnp.sum(
                delta_s[:, mine].astype(jnp.float32), axis=0, keepdims=True
            )
            dout_ref[h] += jnp.sum(
                err * act2_s[:, mine].astype(jnp.float32), axis=0, keepdims=True
            )
            return carry

        return lax.fori_loop(0, heads, head, carry)

    lax.fori_loop(0, n, step, 0)

    stage[...] = acc_in[...].astype(jnp.bfloat16)
    dmid_ref[...] = acc_mid[...].astype(jnp.bfloat16)
    for d in range(1, n):
        send_in(d).start()
    for h in range(heads):
        din_ref[h, :, mine] = acc_in[h, pl.ds(pl.multiple_of(me * fs, fs), fs), :]
    for d in range(1, e):
        send_q(d).wait_recv()
    q_min = qmin_s[...]
    for d in range(1, e):
        q_min = jnp.minimum(q_min, qbuf[d])
    gap = q_min - vnow_ref[...]
    vg_ref[...] = -2.0 * jnp.where(gap < 0.0, 0.3, 0.7) * gap
    for d in range(1, n):
        send_in(d).wait_recv()
        owner = lax.rem(me + n - d, n)
        for h in range(heads):
            din_ref[h, :, pl.ds(pl.multiple_of(owner * ks, ks), ks)] = ibuf[d, h].astype(
                jnp.float32
            )
    for d in range(1, n):
        send_x(d).wait_send()
        send_t(d).wait_send()
        send_in(d).wait_send()
    for d in range(1, e):
        send_q(d).wait_send()


def per_device(
    n, e, features, reward, done, value_next, value_now, w_in, w_mid, biases, w_out
):
    rows, feats = features.shape
    heads, _, units = w_in.shape
    ks, fs = units // n, feats // n
    f32, bf16 = jnp.float32, jnp.bfloat16
    vmem = pl.BlockSpec(memory_space=pltpu.VMEM)
    dma = pltpu.SemaphoreType.DMA
    vg, d_in, d_mid, d_bias, d_out = pl.pallas_call(
        functools.partial(kernel, n, e),
        out_shape=(
            jax.ShapeDtypeStruct((1, rows), f32),
            jax.ShapeDtypeStruct((heads, fs, units), f32),
            jax.ShapeDtypeStruct((heads, ks, units), bf16),
            jax.ShapeDtypeStruct((2, heads, 1, ks), f32),
            jax.ShapeDtypeStruct((heads, 1, ks), f32),
        ),
        in_specs=[vmem] * 6 + [pl.BlockSpec(memory_space=pl.ANY)] + [vmem] * 2,
        out_specs=(vmem,) * 5,
        scratch_shapes=[
            pltpu.VMEM((heads, units, units), bf16),
            pltpu.VMEM((heads, units, ks), bf16),
            pltpu.VMEM((n, rows, feats), bf16),
            pltpu.VMEM((n, 1, rows), f32),
            pltpu.VMEM((rows, units), bf16),
            pltpu.VMEM((rows, units), bf16),
            pltpu.VMEM((rows, units), f32),
            pltpu.VMEM((rows, units), bf16),
            pltpu.VMEM((heads, ks, units), f32),
            pltpu.VMEM((heads, feats, ks), f32),
            pltpu.VMEM((heads, feats, ks), bf16),
            pltpu.VMEM((n, heads, fs, ks), bf16),
            pltpu.VMEM((1, rows), f32),
            pltpu.VMEM((e, 1, rows), f32),
            dma((heads,)),
            dma((n,)), dma((n,)), dma((n,)), dma((n,)), dma((n,)), dma((n,)),
            dma((e,)), dma((e,)),
        ],
        compiler_params=pltpu.CompilerParams(
            collective_id=0, has_side_effects=True, vmem_limit_bytes=62 * 1024 * 1024
        ),
    )(
        features, reward[None], done[None], value_next[None], value_now[None], w_in, w_mid,
        biases[:, :, None, :], w_out.astype(f32)[:, None, :],
    )
    return (
        vg[0],
        jnp.transpose(d_in, (1, 0, 2)),
        jnp.transpose(d_mid, (1, 0, 2)).astype(f32),
        d_bias[:, :, 0, :],
        d_out[:, 0, :],
    )


def solution(mesh):
    in_specs = (
        P("dp", None),
        P("dp"),
        P("dp"),
        P("dp"),
        P("dp"),
        P("ens", None, None),
        P("ens", None, None),
        P(None, "ens", None),
        P("ens", None),
    )
    out_specs = (
        P("dp"),
        P("dp", "ens", None),
        P("dp", "ens", None),
        P(None, "ens", "dp"),
        P("ens", "dp"),
    )
    body = functools.partial(per_device, mesh.shape["dp"], mesh.shape["ens"])
    return jax.shard_map(
        body, mesh=mesh, in_specs=in_specs, out_specs=out_specs, check_vma=False
    )
```

time: 562 us -> 152 us (0.27)
  waiting for transfers between devices: 457 us -> 0 us
  Pallas kernels: 0 us -> 133 us
  matrix products: 52.7 us -> 0 us
  between operations: 14.6 us -> 0.69 us
  blocking collectives: 8.34 us -> 0 us
  other arithmetic: 9.62 us -> 2.7 us
    reduce_scatter x1 -> x0, waiting for transfers between devices: 281 us -> none  [per_device(): lax.psum_scatter(grad_mid.astype(jnp.bfloat16), 'dp', scatter_dimension=0...]
    unnamed x7 -> x0, waiting for transfers between devices: 176 us -> none
    pallas_call x0 -> x1, Pallas kernels: none -> 133 us  [per_device(): pl.pallas_call(functools.partial(kernel, n, e), out_shape=(jax.ShapeDtype...]
    dot_general x7 -> x0, matrix products: 52.7 us -> none  [the longest x1 15.8 us: per_device(): jnp.einsum('hrk,hrj->khj', act_one, delta_two, preferred_element_type=jnp...]
    pmin x1 -> x0, blocking collectives: 8.34 us -> none  [per_device(): q_min = lax.pmin(jnp.min(q_values, axis=0), 'ens')]
    broadcast_in_dim x0 -> x6, local copies, waits for them, and re-layouts: none -> 7.72 us  [the longest x1 1.4 us: per_device(): biases[:, :, None, :]]
    unnamed x28 -> x12, local copies, waits for them, and re-layouts: 13.6 us -> 7.64 us
    reduce_sum x1 -> x0, other arithmetic: 5.73 us -> none  [per_device(): grad_two = jnp.sum(delta_two.astype(jnp.float32), axis=1)]
  transfers between devices with their start and end apart: 4 -> 0, of which waited for: 4 -> 0; matrix products, arithmetic and copies ran while one was open for 9% -> 0% of each run, Pallas kernels for 0% -> 0%
where the time goes in v1:
time: 152 us
  Pallas kernels  133 us (88%)
  local copies, waits for them, and re-layouts  15.4 us (10%)
  other arithmetic  2.7 us (2%)
    pallas_call x1, Pallas kernels, per_device(): pl.pallas_call(functools.partial(kernel, n, e), out_shape=(jax.ShapeDtype...  133 us
    unnamed x12, local copies, waits for them, and re-layouts  7.64 us

profile of v1, /device:TPU:0, one launch (start us, length us, event | category | flops | bytes accessed | tf_op | source)
XLA Modules:
  0.0 152.1 jit_solution(4258501605171853621)
XLA Ops:
  0.6 1.4 broadcast_in_dim.24.bias_ref
  2.0 1.3 reshape.10.w_out_ref
  3.3 1.2 broadcast_in_dim.20.reward_ref
  4.6 1.2 broadcast_in_dim.21.done_ref
  5.8 1.2 broadcast_in_dim.22.vnext_ref
  7.1 1.3 broadcast_in_dim.23.vnow_ref
  8.3 133.3 %shard_map.128 = (f32[1,384]{1,0:T(1,128)}, f32[2,32,2048]{2,1,0:T(8,128)}, bf16[2,256,2048]{2,1,0:T(8,128)(2,1)}, f32[2,2,1,256]{3,2,1,0:T(1,128)}, f32[2,1,256]{2,1,0:T(1,128)}) custom-call(bf16[384,256]{1,0:T(8,128)(2,1)} %x_ref.1, f32[1,384]{1,0:T(1,128)} %broadcast_in_dim.20.reward_ref, s32[1,384]{1,0:T(1,128)} %broadcast_in_dim.21.done_ref, ...), custom_call_target="tpu_custom_call" | custom-call | tf_op jit(solution)/shard_map/pallas_call | solution.py:200
  141.7 2.1 %convert_bitcast_fusion = f32[256,2,2048]{2,0,1:T(8,128)S(1)} fusion(bf16[2,256,2048]{2,1,0:T(8,128)(2,1)} %get-tuple-element.12), kind=kLoop, calls=%fused_computation | loop fusion | flops 1048576 | bytes 6291456 | tf_op jit(solution)/shard_map/convert_element_type | solution.py:240
  143.8 0.0 copy-start
  143.8 0.0 copy-start.1
  143.8 0.0 copy-start.2
  143.9 0.0 copy-start.3
  143.9 5.2 %copy.15 = f32[256,2,2048]{2,1,0:T(2,128)} copy(f32[256,2,2048]{2,0,1:T(8,128)S(1)} %convert_bitcast_fusion) | data formatting | bytes 8388608
  149.1 0.0 copy-done
  149.1 1.2 copy.14
  150.3 0.0 copy-done.1
  150.3 0.6 copy.20
  150.9 0.0 copy-done.2
  150.9 0.6 copy.21
  151.5 0.0 copy-done.3
  151.5 0.6 reduce
Async XLA Ops:
  143.8 5.3 %copy-start = (f32[2,32,2048]{2,1,0:T(8,128)S(1)}, f32[2,32,2048]{2,1,0:T(8,128)}, u32[]{:S(2)}) copy-start(f32[2,32,2048]{2,1,0:T(8,128)} %get-tuple-element.11) | copy-start | bytes 1572868
  143.8 6.5 %copy-start.1 = (f32[2,2,1,256]{3,2,1,0:T(1,128)S(1)}, f32[2,2,1,256]{3,2,1,0:T(1,128)}, u32[]{:S(2)}) copy-start(f32[2,2,1,256]{3,2,1,0:T(1,128)} %get-tuple-element.13) | copy-start | bytes 12292
  143.8 7.1 %copy-start.2 = (f32[2,1,256]{2,1,0:T(1,128)S(1)}, f32[2,1,256]{2,1,0:T(1,128)}, u32[]{:S(2)}) copy-start(f32[2,1,256]{2,1,0:T(1,128)} %get-tuple-element.14) | copy-start | bytes 6148
  143.9 7.6 %copy-start.3 = (f32[1,384]{1,0:T(1,128)S(1)}, f32[1,384]{1,0:T(1,128)}, u32[]{:S(2)}) copy-start(f32[1,384]{1,0:T(1,128)} %get-tuple-element.10) | copy-start | bytes 4612
